TPU v7x, 8 devices: a whole 2x2x1 slice. The times are simulated.
8 devices in a mesh: ez: 2 (over z, y), ey: 2 (over x), ex: 2 (over core).
Axes of the slice: x: 2, y: 2, z: 1, core: 2. Of those that a mesh axis runs over, the one named last changes fastest.
Arguments:
- x_tokens: bfloat16 [512, 2048], P(('ez', 'ey', 'ex'))
- expert_ids: int32 [512, 8], P(('ez', 'ey', 'ex'))
- gate_vals: float32 [512, 8], P(('ez', 'ey', 'ex'))
- w_gate: bfloat16 [64, 2048, 1024], P(('ex', 'ey', 'ez'))
- w_up: bfloat16 [64, 2048, 1024], P(('ex', 'ey', 'ez'))
- w_down: bfloat16 [64, 1024, 2048], P(('ex', 'ey', 'ez'))
Outputs:
- output: bfloat16 [512, 2048], P(('ez', 'ey', 'ex'))
All inputs are finite; a program needn't handle non-finite values.
Results may differ from a plain program's by a relative error of at most 0.00108.
Values are sent between devices in bfloat16 or wider.
A program may use at most 1 GiB of HBM per device.

v0:
```python
import jax
import jax.numpy as jnp
from jax import lax
from jax.sharding import PartitionSpec as P

TOKEN_AXES = ('ez', 'ey', 'ex')
EXPERT_AXES = ('ex', 'ey', 'ez')


def slot_layout(ids_local, n_exp, cap_slot):
    tok_dev, top_k = ids_local.shape
    flat_ids = ids_local.reshape(-1)
    match_mat = (flat_ids[:, None] == jnp.arange(n_exp)[None, :]).astype(jnp.int32)
    slot_rank = jnp.sum(jnp.cumsum(match_mat, axis=0) * match_mat, axis=1) - 1
    slot_idx = flat_ids * cap_slot + slot_rank
    pair_tok = jnp.arange(tok_dev * top_k, dtype=jnp.int32) // top_k
    slot_tok = jnp.zeros((n_exp * cap_slot,), jnp.int32).at[slot_idx].set(pair_tok)
    return slot_idx, slot_tok


def solution(mesh):
    n_dev = mesh.shape['ez'] * mesh.shape['ey'] * mesh.shape['ex']

    def local_layer(x_loc, ids_loc, gates_loc, w_g, w_u, w_d):
        tok_dev, hid_dim = x_loc.shape
        top_k = ids_loc.shape[1]
        n_local = w_g.shape[0]
        n_exp = n_local * n_dev
        cap_slot = 2 * tok_dev * top_k // n_exp
        slot_idx, slot_tok = slot_layout(ids_loc, n_exp, cap_slot)
        send_buf = jnp.take(x_loc, slot_tok, axis=0).reshape(n_dev, n_local, cap_slot, hid_dim)
        recv_buf = lax.all_to_all(send_buf, EXPERT_AXES, 0, 0)
        h_gate = jnp.einsum('slch,lhf->slcf', recv_buf, w_g, preferred_element_type=jnp.float32)
        h_up = jnp.einsum('slch,lhf->slcf', recv_buf, w_u, preferred_element_type=jnp.float32)
        act_bf = (jax.nn.silu(h_gate) * h_up).astype(jnp.bfloat16)
        exp_out = jnp.einsum('slcf,lfh->slch', act_bf, w_d, preferred_element_type=jnp.float32).astype(jnp.bfloat16)
        back_buf = lax.all_to_all(exp_out, EXPERT_AXES, 0, 0)
        back_flat = back_buf.reshape(n_exp * cap_slot, hid_dim)
        tok_rows = jnp.take(back_flat, slot_idx, axis=0).reshape(tok_dev, top_k, hid_dim)
        moe_sum = jnp.sum(gates_loc[:, :, None] * tok_rows, axis=1)
        return (x_loc.astype(jnp.float32) + moe_sum).astype(jnp.bfloat16)

    tok_spec = P(TOKEN_AXES, None)
    w_spec = P(EXPERT_AXES, None, None)
    return jax.shard_map(local_layer, mesh=mesh, in_specs=(tok_spec, tok_spec, tok_spec, w_spec, w_spec, w_spec), out_specs=tok_spec, check_vma=False)
```

profile of v0, /device:TPU:0, one launch (start us, length us, event | category | flops | bytes accessed | tf_op | source)
XLA Modules:
  0.0 185.5 jit_solution(6929309092388458662)
XLA Ops:
  0.0 0.0 copy-start
  0.0 0.8 copy.26
  0.8 0.1 eq.26
  0.9 0.1 reshape.85
  1.0 0.7 broadcast_multiply_fusion
  1.7 1.2 reduce-window.6
  2.9 0.2 slice_reduce_fusion
  3.2 0.1 fusion.19
  3.3 0.1 copy.31
  3.4 0.1 mul.41
  3.5 2.4 %scatter_custom_fusion = s32[1024]{0:T(1024)S(1)} fusion(s32[512]{0:T(512)S(1)} %bitcast.64, s32[512]{0:T(512)S(1)} %add_select_fusion, s32[]{:T(128)} %constant.52.clone.1), kind=kCustom, calls=%fused_computation.44 | custom fusion | bytes 4100 | tf_op jit(solution)/shard_map/scatter | solution.py:17
  6.0 0.1 broadcast_in_dim.32
  6.1 0.0 copy-done
  6.1 6.0 %gather_fusion = bf16[1024,2048]{1,0:T(8,128)(2,1)} fusion(bf16[64,2048]{1,0:T(8,128)(2,1)S(1)} %copy-done, s32[1024]{0:T(1024)S(1)} %fusion.21), kind=kCustom, calls=%fused_computation | custom fusion | bytes 8392704 | tf_op jit(solution)/shard_map/jit(_take)/gather | solution.py:31
  12.1 2.6 %broadcast_select_fusion = bf16[8,8,16,2048]{3,2,1,0:T(8,128)(2,1)S(1)} fusion(bf16[8,8,16,2048]{3,2,1,0:T(8,128)(2,1)} %bitcast.62, pred[8,8,16]{2,1,0:T(8,128)(4,1)S(1)} %broadcast_in_dim.32), kind=kLoop, calls=%fused_computation.18 | loop fusion | flops 2097152 | bytes 8389632 | tf_op jit(solution)/shard_map/jit(_take)/select_n | solution.py:31
  14.8 52.8 %all_to_all.10 = bf16[8,8,16,2048]{3,2,1,0:T(8,128)(2,1)} all-to-all(bf16[8,8,16,2048]{3,2,1,0:T(8,128)(2,1)S(1)} %broadcast_select_fusion), channel_id=1, replica_groups=mesh['ez'=2,'ey'=2,'ex'=2] {'ex','ey','ez'}, dimensions={0} | all-to-all | bytes 8388608 | tf_op jit(solution)/shard_map/all_to_all | solution.py:32
  67.5 18.3 %fusion.2 = f32[8,8,16,1024]{3,2,1,0:T(8,128)} fusion(bf16[8,2048,1024]{2,1,0:T(8,128)(2,1)} %param.10, bf16[8,8,16,2048]{3,2,1,0:T(8,128)(2,1)} %all_to_all.10), kind=kOutput, calls=%fused_computation.5 | convolution fusion | flops 4294967296 | bytes 41943040 | tf_op jit(solution)/shard_map/slch,lhf->slcf/dot_general | solution.py:34
  85.9 15.8 %fusion.6 = bf16[8,8,16,1024]{3,2,0,1:T(8,128)(2,1)S(1)} fusion(f32[8,8,16,1024]{3,2,1,0:T(8,128)} %fusion.2, bf16[8,2048,1024]{2,1,0:T(8,128)(2,1)} %param.9, bf16[8,8,16,2048]{3,2,1,0:T(8,128)(2,1)} %all_to_all.10), kind=kOutput, calls=%fused_computation.10 | convolution fusion | flops 4301258752 | bytes 44040192 | tf_op jit(solution)/shard_map/slch,lhf->slcf/dot_general | solution.py:33
  101.7 17.1 %convert_bitcast_fusion = bf16[8,8,16,2048]{3,2,0,1:T(8,128)(2,1)} fusion(bf16[8,8,16,1024]{3,2,0,1:T(8,128)(2,1)S(1)} %fusion.6, bf16[8,1024,2048]{2,1,0:T(8,128)(2,1)} %param.11), kind=kOutput, calls=%fused_computation.17 | convolution fusion | flops 4297064448 | bytes 39845888 | tf_op jit(solution)/shard_map/slcf,lfh->slch/dot_general | solution.py:36
  118.8 4.7 %copy.34 = bf16[8,8,16,2048]{3,2,1,0:T(8,128)(2,1)} copy(bf16[8,8,16,2048]{3,2,0,1:T(8,128)(2,1)} %convert_bitcast_fusion) | data formatting | bytes 8388608 | tf_op jit(solution)/shard_map/convert_element_type | solution.py:36
  123.5 0.0 copy-start.1
  123.5 3.4 %all-to-all-start.1 = ((bf16[8,8,16,2048]{3,2,1,0:T(8,128)(2,1)}), bf16[8,8,16,2048]{3,2,1,0:T(8,128)(2,1)}, u32[]{:S(2)}, u32[]{:S(2)}) async-start(bf16[8,8,16,2048]{3,2,1,0:T(8,128)(2,1)} %copy.34), calls=%async_computation.1 | async-start | bytes 8388608 | tf_op jit(solution)/shard_map/all_to_all | solution.py:37
  126.9 0.1 sub.15
  127.0 0.1 copy.29
  127.0 0.0 copy-done.1
  127.1 0.1 copy.30
  127.2 0.0 copy-done.2
  127.2 0.1 copy.25
  127.3 47.8 %all-to-all-done.1 = bf16[8,8,16,2048]{3,2,1,0:T(8,128)(2,1)} async-done(((bf16[8,8,16,2048]{3,2,1,0:T(8,128)(2,1)}), bf16[8,8,16,2048]{3,2,1,0:T(8,128)(2,1)}, u32[]{:S(2)}, u32[]{:S(2)}) %all-to-all-start.1) | async-done | bytes 4194336 | tf_op jit(solution)/shard_map/all_to_all | solution.py:37
  175.1 7.1 %gather_fusion.1 = bf16[512,2048]{1,0:T(8,128)(2,1)S(1)} fusion(bf16[1024,2048]{1,0:T(8,128)(2,1)} %bitcast.13, s32[1024]{0:T(1024)S(1)} %pad_clamp_fusion), kind=kCustom, calls=%fused_computation.1 | custom fusion | bytes 4196352 | tf_op jit(solution)/shard_map/jit(_take)/gather | solution.py:39
  182.2 2.5 %multiply_reduce_fusion = f32[64,2048]{1,0:T(8,128)S(1)} fusion(bf16[512,2048]{1,0:T(8,128)(2,1)S(1)} %gather_fusion.1, f32[64,8]{1,0:T(8,128)S(1)} %copy.25, pred[64,8]{1,0:T(8,128)(4,1)S(1)} %copy.30), kind=kLoop, calls=%fused_computation.16 | loop fusion | flops 4063232 | bytes 2624000 | tf_op jit(solution)/shard_map/reduce_sum | solution.py:40
  184.7 0.8 add_convert_fusion
  (11 shorter events, 0.1 us)
Async XLA Ops:
  0.0 6.1 %copy-start = (bf16[64,2048]{1,0:T(8,128)(2,1)S(1)}, bf16[64,2048]{1,0:T(8,128)(2,1)}, u32[]{:S(2)}) copy-start(bf16[64,2048]{1,0:T(8,128)(2,1)} %param.6) | copy-start | bytes 786436
  123.5 3.6 %copy-start.1 = (s32[64,8]{0,1:T(8,128)S(1)}, s32[64,8]{0,1:T(8,128)}, u32[]{:S(2)}) copy-start(s32[64,8]{0,1:T(8,128)} %param.7) | copy-start | bytes 6148
  123.5 3.7 %copy-start.2 = (f32[64,8]{0,1:T(8,128)S(1)}, f32[64,8]{0,1:T(8,128)}, u32[]{:S(2)}) copy-start(f32[64,8]{0,1:T(8,128)} %param.8) | copy-start | bytes 6148
  123.5 51.6 %all-to-all-start.1 = ((bf16[8,8,16,2048]{3,2,1,0:T(8,128)(2,1)}), bf16[8,8,16,2048]{3,2,1,0:T(8,128)(2,1)}, u32[]{:S(2)}, u32[]{:S(2)}) async-start(bf16[8,8,16,2048]{3,2,1,0:T(8,128)(2,1)} %copy.34), calls=%async_computation.1 | async-start | bytes 8388608 | tf_op jit(solution)/shard_map/all_to_all | solution.py:37
where the time goes:
time: 186 us; the launch traced here: 185 us
  blocking collectives  52.8 us (28%)
  matrix products  51.2 us (28%)
  waiting for transfers between devices  47.8 us (26%)
  local copies, waits for them, and re-layouts  22.1 us (12%)
  other arithmetic  8.04 us (4%)
  starting transfers between devices  3.41 us (2%)
    all_to_all x1, blocking collectives, local_layer(): recv_buf = lax.all_to_all(send_buf, EXPERT_AXES, 0, 0)  52.8 us
    all_to_all x1, waiting for transfers between devices, local_layer(): back_buf = lax.all_to_all(exp_out, EXPERT_AXES, 0, 0)  47.8 us
    dot_general x1, matrix products, local_layer(): jnp.einsum('slch,lhf->slcf', recv_buf, w_u, preferred_element_type=jnp.fl...  18.3 us
    dot_general x1, matrix products, local_layer(): jnp.einsum('slcf,lfh->slch', act_bf, w_d, preferred_element_type=jnp.floa...  17.1 us
    dot_general x1, matrix products, local_layer(): jnp.einsum('slch,lhf->slcf', recv_buf, w_g, preferred_element_type=jnp.fl...  15.8 us
    gather x1, local copies, waits for them, and re-layouts, local_layer(): jnp.take(back_flat, slot_idx, axis=0).reshape(tok_dev, top_k, hid_dim)  7.13 us
    gather x1, local copies, waits for them, and re-layouts, local_layer(): jnp.take(x_loc, slot_tok, axis=0).reshape(n_dev, n_local, cap_slot, hid_dim)  6.02 us
    convert_element_type x1, local copies, waits for them, and re-layouts, local_layer(): jnp.einsum('slcf,lfh->slch', act_bf, w_d, preferred_element_type=jnp.floa...  4.7 us
  transfers between devices with their start and end apart: 1, of which 1 were waited for; matrix products, arithmetic and copies ran while one was open for 0% of the time, Pallas kernels for 0%

commit v1 on v0

v1 whole, which is shorter than its diff:
```python
import jax
import jax.numpy as jnp
from jax import lax
from jax.experimental import pallas as pl
from jax.experimental.pallas import tpu as pltpu
from jax.sharding import PartitionSpec as P

TOKEN_AXES = ('ez', 'ey', 'ex')
EXPERT_AXES = ('ex', 'ey', 'ez')
MESH = pl.DeviceIdType.MESH
F32 = jnp.float32
BF16 = jnp.bfloat16

TOK = 64
HID = 2048
FFN = 1024
NEXP = 8
CAP = 16
NSLOT = 10
CB = 256
NCB = HID // CB
N13 = 2 * NEXP

PEERS = [(c, s) for c in range(4) for s in range(2) if (c, s) != (0, 0)]


def kernel(x_hbm, ids_hbm, gates_hbm, wg_hbm, wu_hbm, wd_hbm, y_hbm,
           ring, xs, xe, act, acc, dsend, drecv, r2, f3, r3, pmat, gtmp, gmat, obuf, ids_v, gates_v, meta, yv,
           w_sem, loc_sem, xsend, xrecv, fsend, msend, mrecv, d_send, d_recv, s2_send, s2_recv, s3_send, s3_recv, y_sem):
    ez, ey, ex = lax.axis_index('ez'), lax.axis_index('ey'), lax.axis_index('ex')

    def dev(c, s):
        return (1 - ez if c & 2 else ez, 1 - ey if c & 1 else ey, 1 - ex if s else ex)

    def remote(src, dst, ssem, rsem, c, s):
        return pltpu.make_async_remote_copy(src_ref=src, dst_ref=dst, send_sem=ssem, recv_sem=rsem,
                                            device_id=dev(c, s), device_id_type=MESH)

    cp_x = pltpu.make_async_copy(x_hbm, xs.at[0, pl.ds(0, TOK)], loc_sem.at[0])
    cp_i = pltpu.make_async_copy(ids_hbm, ids_v, loc_sem.at[1])
    cp_g = pltpu.make_async_copy(gates_hbm, gates_v, loc_sem.at[2])
    cp_x.start()
    cp_i.start()
    cp_g.start()

    barrier = pltpu.get_barrier_semaphore()
    for c, s in PEERS:
        pl.semaphore_signal(barrier, inc=1, device_id=dev(c, s), device_id_type=MESH)

    def start_w13(w_hbm, e, slot):
        for q in range(4):
            pltpu.make_async_copy(w_hbm.at[e, :, :, pl.ds(q * CB, CB)], ring.at[slot, pl.ds(2 * q, 2)],
                                  w_sem.at[slot]).start()

    def start_w2(cb, slot):
        pltpu.make_async_copy(wd_hbm.at[:, :, pl.ds(pl.multiple_of(cb * CB, CB), CB)], ring.at[slot], w_sem.at[slot]).start()

    def wait_w(slot):
        pltpu.make_async_copy(ring.at[slot], ring.at[slot], w_sem.at[slot]).wait()

    for e in range(NSLOT // 2):
        start_w13(wg_hbm, e, 2 * e)
        start_w13(wu_hbm, e, 2 * e + 1)

    cp_i.wait()
    cp_g.wait()
    ids_f = ids_v[...].astype(F32)
    gates_f = gates_v[...]
    meta[0, 0, 0:8, :] = jnp.concatenate([ids_f, ids_f], axis=1)
    meta[0, 0, 8:16, :] = jnp.concatenate([gates_f, gates_f], axis=1)
    cp_x.wait()
    pl.semaphore_wait(barrier, len(PEERS))

    def rows(c, s, h):
        return xs.at[c, pl.ds(s * TOK + h * (TOK // 2), TOK // 2)]

    sends = []

    def send_rows(src, dst, ssem, c, s):
        cp = remote(rows(*src), rows(*dst), ssem, xrecv.at[dst[0], dst[1], dst[2]], c, s)
        cp.start()
        sends.append(cp)

    def wait_rows(c, s, h):
        remote(rows(c, s, h), rows(c, s, h), fsend.at[0], xrecv.at[c, s, h], 0, 1).wait_recv()

    meta_sends = []
    for i, (c, s) in enumerate(PEERS):
        cp = remote(meta.at[0, 0], meta.at[c, s], msend.at[i], mrecv.at[c, s], c, s)
        cp.start()
        meta_sends.append(cp)
    send_rows((0, 0, 1), (1, 0, 1), xsend.at[0], 1, 0)
    send_rows((0, 0, 0), (2, 0, 0), xsend.at[1], 2, 0)
    send_rows((0, 0, 0), (1, 0, 0), xsend.at[2], 1, 0)
    send_rows((0, 0, 1), (2, 0, 1), xsend.at[3], 2, 0)
    send_rows((0, 0, 0), (0, 1, 0), xsend.at[4], 0, 1)
    send_rows((0, 0, 1), (0, 1, 1), xsend.at[5], 0, 1)

    for c, s in PEERS:
        remote(meta.at[c, s], meta.at[c, s], msend.at[0], mrecv.at[c, s], 0, 1).wait_recv()
    base = ((ex * 2 + ey) * 2 + ez) * NEXP
    sub8 = lax.broadcasted_iota(jnp.int32, (NEXP, 128), 0)
    lane8 = lax.broadcasted_iota(jnp.int32, (NEXP, 128), 1)
    mine = (sub8 + base).astype(F32)
    masks, gates = [], []
    for c in range(4):
        m = jnp.where(lane8[0:1] < TOK, meta[c, 0], meta[c, 1])
        mask = jnp.zeros((NEXP, 128), F32)
        gate = jnp.zeros((NEXP, 128), F32)
        for j in range(8):
            hit = m[j:j + 1, :] == mine
            mask += jnp.where(hit, 1.0, 0.0)
            gate += jnp.where(hit, m[8 + j:9 + j, :], 0.0)
        masks.append(mask)
        gates.append(gate)
    r_i = lax.broadcasted_iota(jnp.int32, (128, 128), 0)
    c_i = lax.broadcasted_iota(jnp.int32, (128, 128), 1)
    before = jnp.where((r_i < c_i) & ((r_i < TOK) == (c_i < TOK)), 1.0, 0.0).astype(BF16)
    rank = jnp.dot(jnp.concatenate(masks, axis=0).astype(BF16), before, preferred_element_type=F32)
    sub32 = lax.broadcasted_iota(jnp.int32, (2 * CAP, 128), 0).astype(F32)
    core_off = jnp.where(lane8 < TOK, 0.0, float(CAP))
    for c in range(4):
        code = jnp.where(masks[c] > 0.5, rank[c * NEXP:(c + 1) * NEXP] + core_off, -1.0)
        for e in range(NEXP):
            hit = sub32 == code[e:e + 1, :]
            pmat[c, 2 * CAP * e:2 * CAP * (e + 1), :] = jnp.where(hit, 1.0, 0.0).astype(BF16)
            gtmp[c, 2 * CAP * e:2 * CAP * (e + 1), :] = jnp.where(hit, gates[c][e:e + 1, :], 0.0)
    for c in range(4):
        gt = gtmp[c].T
        hi = gt.astype(BF16)
        rest = gt - hi.astype(F32)
        mid = rest.astype(BF16)
        gmat[c, 0:128, :] = hi
        gmat[c, 128:256, :] = mid
        gmat[c, 256:384, :] = (rest - mid.astype(F32)).astype(BF16)

    def gather(c):
        for nb in range(HID // 512):
            cols = slice(nb * 512, (nb + 1) * 512)
            blk = jnp.dot(pmat[c], xs[c, :, cols], preferred_element_type=F32).astype(BF16)
            for e in range(NEXP):
                xe[e, 2 * CAP * c:2 * CAP * (c + 1), cols] = blk[2 * CAP * e:2 * CAP * (e + 1)]

    wait_rows(1, 0, 1)
    send_rows((1, 0, 1), (3, 0, 1), fsend.at[0], 2, 0)
    send_rows((1, 0, 1), (1, 1, 1), fsend.at[1], 0, 1)
    wait_rows(2, 0, 0)
    send_rows((2, 0, 0), (3, 0, 0), fsend.at[2], 1, 0)
    send_rows((2, 0, 0), (2, 1, 0), fsend.at[3], 0, 1)
    wait_rows(0, 1, 0)
    wait_rows(0, 1, 1)
    gather(0)
    wait_rows(1, 0, 0)
    send_rows((1, 0, 0), (1, 1, 0), fsend.at[4], 0, 1)
    wait_rows(2, 0, 1)
    send_rows((2, 0, 1), (2, 1, 1), fsend.at[5], 0, 1)
    wait_rows(1, 1, 0)
    wait_rows(1, 1, 1)
    gather(1)
    wait_rows(2, 1, 0)
    wait_rows(2, 1, 1)
    gather(2)
    wait_rows(3, 0, 0)
    send_rows((3, 0, 0), (3, 1, 0), fsend.at[6], 0, 1)
    wait_rows(3, 0, 1)
    send_rows((3, 0, 1), (3, 1, 1), fsend.at[7], 0, 1)
    wait_rows(3, 1, 0)
    wait_rows(3, 1, 1)
    gather(3)

    def up(e, carry):
        s1 = lax.rem(2 * e, NSLOT)
        s3 = lax.rem(2 * e + 1, NSLOT)
        wait_w(s1)
        wait_w(s3)
        for q in range(4):
            xin = xe[e]
            h1 = jnp.dot(xin, ring[s1, 2 * q:2 * q + 2].reshape(HID, CB), preferred_element_type=F32)
            h3 = jnp.dot(xin, ring[s3, 2 * q:2 * q + 2].reshape(HID, CB), preferred_element_type=F32)
            act[e, :, q * CB:(q + 1) * CB] = (jax.nn.silu(h1) * h3).astype(BF16)

        @pl.when(e < NEXP - NSLOT // 2)
        def _():
            start_w13(wg_hbm, e + NSLOT // 2, s1)
            start_w13(wu_hbm, e + NSLOT // 2, s3)

        @pl.when((e >= NEXP - NSLOT // 2) & (e < NEXP - 1))
        def _():
            cb = 2 * (e - (NEXP - NSLOT // 2))
            start_w2(cb, s1)
            start_w2(cb + 1, s3)

        return carry

    lax.fori_loop(0, NEXP, up, 0)

    def part(cb):
        slot = lax.rem(N13 + cb, NSLOT)
        wait_w(slot)
        for e in range(NEXP):
            o = jnp.dot(act[e], ring[slot, e], preferred_element_type=F32).astype(BF16)
            for c in range(4):
                obuf[c, 2 * CAP * e:2 * CAP * (e + 1), :] = o[2 * CAP * c:2 * CAP * (c + 1)]
        for c in range(4):
            t = jnp.dot(gmat[c], obuf[c], preferred_element_type=F32)
            t = t[0:128] + t[128:256] + t[256:384]
            acc[cb, c] = t[0:TOK]
            dsend[cb, c] = t[TOK:2 * TOK]
        remote(dsend.at[cb], drecv.at[cb], d_send.at[cb], d_recv.at[cb], 0, 1).start()

    def first(odd):
        return (2, 1) if odd else (1, 2)

    def s2_copies(cb, odd):
        a, b = first(odd)
        return [remote(acc.at[cb, a], r2.at[cb, 0], s2_send.at[cb, 0], s2_recv.at[cb, 0], a, 0),
                remote(acc.at[cb, 3], r2.at[cb, 1], s2_send.at[cb, 1], s2_recv.at[cb, 1], a, 0)]

    def stage2(cb, odd):
        remote(dsend.at[cb], drecv.at[cb], d_send.at[cb], d_recv.at[cb], 0, 1).wait_recv()
        acc[cb] = acc[cb] + drecv[cb]
        cps = s2_copies(cb, odd)
        cps[1].start()
        cps[0].start()

    def s3_copy(cb, odd):
        a, b = first(odd)
        return remote(f3.at[cb], r3.at[cb], s3_send.at[cb], s3_recv.at[cb], b, 0)

    def stage3(cb, odd):
        a, b = first(odd)
        s2_copies(cb, odd)[1].wait_recv()
        f3[cb] = acc[cb, b] + r2[cb, 1]
        s3_copy(cb, odd).start()

    def y_copy(cb):
        cols = pl.ds(pl.multiple_of(cb * CB, CB), CB)
        return pltpu.make_async_copy(yv.at[cb], y_hbm.at[:, cols], y_sem.at[cb])

    def final(cb, odd):
        s2_copies(cb, odd)[0].wait_recv()
        s3_copy(cb, odd).wait_recv()
        cols = pl.ds(pl.multiple_of(cb * CB, CB), CB)
        xin = xs[0, 0:TOK, cols].astype(F32)
        yv[cb] = (xin + ((acc[cb, 0] + r2[cb, 0]) + r3[cb])).astype(BF16)
        y_copy(cb).start()

    def down(i, carry):
        part(2 * i)

        @pl.when(i > 0)
        def _():
            stage2(2 * i - 1, 1)

        part(2 * i + 1)
        stage2(2 * i, 0)
        return carry

    lax.fori_loop(0, NCB // 2, down, 0)
    stage2(NCB - 1, 1)

    def third(i, carry):
        stage3(2 * i, 0)
        stage3(2 * i + 1, 1)
        return carry

    lax.fori_loop(0, NCB // 2, third, 0)

    def last(i, carry):
        final(2 * i, 0)
        final(2 * i + 1, 1)
        return carry

    lax.fori_loop(0, NCB // 2, last, 0)

    for cp in sends + meta_sends:
        cp.wait_send()
    for cb in range(NCB):
        remote(dsend.at[cb], drecv.at[cb], d_send.at[cb], d_recv.at[cb], 0, 1).wait_send()
        for cp in s2_copies(cb, cb & 1):
            cp.wait_send()
        s3_copy(cb, cb & 1).wait_send()
        y_copy(cb).wait()


def solution(mesh):
    def local_layer(x_loc, ids_loc, gates_loc, w_g, w_u, w_d):
        w_g = w_g.reshape(NEXP, 2, FFN, FFN)
        w_u = w_u.reshape(NEXP, 2, FFN, FFN)
        any_spec = pl.BlockSpec(memory_space=pl.ANY)
        dma = pltpu.SemaphoreType.DMA
        return pl.pallas_call(
            kernel,
            out_shape=jax.ShapeDtypeStruct((TOK, HID), BF16),
            in_specs=[any_spec] * 6,
            out_specs=any_spec,
            scratch_shapes=[
                pltpu.VMEM((NSLOT, NEXP, FFN, CB), BF16),
                pltpu.VMEM((4, 2 * TOK, HID), BF16),
                pltpu.VMEM((NEXP, 8 * CAP, HID), BF16),
                pltpu.VMEM((NEXP, 8 * CAP, FFN), BF16),
                pltpu.VMEM((NCB, 4, TOK, CB), F32),
                pltpu.VMEM((NCB, 4, TOK, CB), F32),
                pltpu.VMEM((NCB, 4, TOK, CB), F32),
                pltpu.VMEM((NCB, 2, TOK, CB), F32),
                pltpu.VMEM((NCB, TOK, CB), F32),
                pltpu.VMEM((NCB, TOK, CB), F32),
                pltpu.VMEM((4, 2 * CAP * NEXP, 128), BF16),
                pltpu.VMEM((4, 2 * CAP * NEXP, 128), F32),
                pltpu.VMEM((4, 384, 2 * CAP * NEXP), BF16),
                pltpu.VMEM((4, 2 * CAP * NEXP, CB), BF16),
                pltpu.VMEM((8, TOK), jnp.int32),
                pltpu.VMEM((8, TOK), F32),
                pltpu.VMEM((4, 2, 16, 128), F32),
                pltpu.VMEM((NCB, TOK, CB), BF16),
                dma((NSLOT,)),
                dma((3,)),
                dma((6,)),
                dma((4, 2, 2)),
                dma((8,)),
                dma((7,)),
                dma((4, 2)),
                dma((NCB,)),
                dma((NCB,)),
                dma((NCB, 2)),
                dma((NCB, 2)),
                dma((NCB,)),
                dma((NCB,)),
                dma((NCB,)),
            ],
            compiler_params=pltpu.CompilerParams(collective_id=0, has_side_effects=True,
                                                 vmem_limit_bytes=67043328),
            name='moe_decode',
        )(x_loc, ids_loc.T, gates_loc.T, w_g, w_u, w_d)

    tok_spec = P(TOKEN_AXES, None)
    w_spec = P(EXPERT_AXES, None, None)
    return jax.shard_map(local_layer, mesh=mesh, in_specs=(tok_spec, tok_spec, tok_spec, w_spec, w_spec, w_spec), out_specs=tok_spec, check_vma=False)
```

time: 186 us -> 54.2 us (0.29)
  blocking collectives: 52.8 us -> 0 us
  Pallas kernels: 0 us -> 52.4 us
  matrix products: 51.2 us -> 0 us
  waiting for transfers between devices: 47.8 us -> 0 us
  local copies, waits for them, and re-layouts: 22.1 us -> 1.67 us
  other arithmetic: 8.04 us -> 0 us
  starting transfers between devices: 3.41 us -> 0 us
    all_to_all x1 -> x0, blocking collectives: 52.8 us -> none  [local_layer(): recv_buf = lax.all_to_all(send_buf, EXPERT_AXES, 0, 0)]
    pallas_call x0 -> x1, Pallas kernels: none -> 52.4 us  [local_layer(): pl.pallas_call(kernel, out_shape=jax.ShapeDtypeStruct((TOK, HID), BF16),...]
    dot_general x3 -> x0, matrix products: 51.2 us -> none  [the longest x1 18.3 us: local_layer(): jnp.einsum('slch,lhf->slcf', recv_buf, w_u, preferred_element_type=jnp.fl...]
    all_to_all x1 -> x0, waiting for transfers between devices: 47.8 us -> none  [local_layer(): back_buf = lax.all_to_all(exp_out, EXPERT_AXES, 0, 0)]
    gather x2 -> x0, local copies, waits for them, and re-layouts: 13.2 us -> none  [the longest x1 7.13 us: local_layer(): jnp.take(back_flat, slot_idx, axis=0).reshape(tok_dev, top_k, hid_dim)]
    convert_element_type x1 -> x0, local copies, waits for them, and re-layouts: 4.7 us -> none  [local_layer(): jnp.einsum('slcf,lfh->slch', act_bf, w_d, preferred_element_type=jnp.floa...]
    all_to_all x1 -> x0, starting transfers between devices: 3.41 us -> none  [local_layer(): back_buf = lax.all_to_all(exp_out, EXPERT_AXES, 0, 0)]
    select_n x3 -> x0, other arithmetic: 2.65 us -> none  [the longest x1 2.63 us: local_layer(): jnp.take(x_loc, slot_tok, axis=0).reshape(n_dev, n_local, cap_slot, hid_dim)]
  transfers between devices with their start and end apart: 1 -> 0, of which waited for: 1 -> 0; matrix products, arithmetic and copies ran while one was open for 0% -> 0% of each run, Pallas kernels for 0% -> 0%
where the time goes in v1:
time: 54.2 us; the launch traced here: 54 us
  Pallas kernels  52.4 us (97%)
  local copies, waits for them, and re-layouts  1.67 us (3%)
    pallas_call x1, Pallas kernels, local_layer(): pl.pallas_call(kernel, out_shape=jax.ShapeDtypeStruct((TOK, HID), BF16),...  52.4 us
    unnamed x1, local copies, waits for them, and re-layouts  1.67 us

profile of v1, /device:TPU:0, one launch (start us, length us, event | category | flops | bytes accessed | tf_op | source)
XLA Modules:
  0.0 54.0 jit_solution(14396421029498221130)
XLA Ops:
  0.0 52.4 %moe_decode.1 = bf16[64,2048]{1,0:T(8,128)(2,1)} custom-call(bf16[64,2048]{1,0:T(8,128)(2,1)} %x_hbm.1, s32[8,64]{1,0:T(8,128)} %bitcast.6, f32[8,64]{1,0:T(8,128)} %bitcast.7, bf16[8,2,1024,1024]{3,2,1,0:T(8,128)(2,1)} %bitcast.4, bf16[8,2,1024,1024]{3,2,1,0:T(8,128)(2,1)} %bitcast.5, bf16[8,1024,2048]{2,1,0:T(8,128)(2,1)} %wd_hbm.1), custom_call_target="tpu_custom_call" | custom-call | tf_op jit(solution)/shard_map/moe_decode/pallas_call | solution.py:292
  52.4 1.7 %copy.8 = bf16[64,2048]{1,0:T(8,128)(2,1)} copy(bf16[64,2048]{1,0:T(8,128)(2,1)} %moe_decode.1) | data formatting | bytes 524288

commit v2 on v0

v2 whole, which is shorter than its diff:
```python
import jax
import jax.numpy as jnp
from jax import lax
from jax.experimental import pallas as pl
from jax.experimental.pallas import tpu as pltpu
from jax.sharding import PartitionSpec as P

TOKEN_AXES = ('ez', 'ey', 'ex')
EXPERT_AXES = ('ex', 'ey', 'ez')
MESH = pl.DeviceIdType.MESH
F32 = jnp.float32
BF16 = jnp.bfloat16

TOK = 64
HALF = TOK // 2
HID = 2048
FFN = 1024
NEXP = 8
CAP = 16
NSLOT = 9
CB = 256
NCB = HID // CB
N13 = 2 * NEXP

PEERS = [(c, s) for c in range(4) for s in range(2) if (c, s) != (0, 0)]
STAY = ((0, 2), (0, 1))
LEAVE = ((1, 3), (2, 3))
HOP1 = (1, 2)
HOP2 = (2, 1)


def kernel(x_hbm, ids_hbm, gates_hbm, wg_hbm, wu_hbm, wd_hbm, y_ref,
           ring, xs, xe, hbuf, act, drecv, r2, r3, pmat, gtmp, gmat, obuf, ids_v, gates_v, meta,
           w_sem, loc_sem, xsend, xrecv, msend, mrecv, d_send, d_recv, s2_send, s2_recv, s3_send, s3_recv):
    ez, ey, ex = lax.axis_index('ez'), lax.axis_index('ey'), lax.axis_index('ex')

    def dev(c, s):
        return (1 - ez if c & 2 else ez, 1 - ey if c & 1 else ey, 1 - ex if s else ex)

    def remote(src, dst, ssem, rsem, c, s):
        return pltpu.make_async_remote_copy(src_ref=src, dst_ref=dst, send_sem=ssem, recv_sem=rsem,
                                            device_id=dev(c, s), device_id_type=MESH)

    cp_x = [pltpu.make_async_copy(x_hbm.at[:, pl.ds(k * FFN, FFN)], xs.at[k, 0, pl.ds(0, TOK)], loc_sem.at[k])
            for k in range(2)]
    cp_i = pltpu.make_async_copy(ids_hbm, ids_v, loc_sem.at[2])
    cp_g = pltpu.make_async_copy(gates_hbm, gates_v, loc_sem.at[3])
    for cp in (cp_x[0], cp_i, cp_g, cp_x[1]):
        cp.start()

    barrier = pltpu.get_barrier_semaphore()
    for c, s in PEERS:
        pl.semaphore_signal(barrier, inc=1, device_id=dev(c, s), device_id_type=MESH)

    def start_w13(k, e, slot):
        for i, w_hbm in enumerate((wg_hbm, wu_hbm)):
            for q in range(4):
                pltpu.make_async_copy(w_hbm.at[e, k, :, pl.ds(q * CB, CB)], ring.at[slot, 4 * i + q],
                                      w_sem.at[slot]).start()

    def start_w2(cb, slot):
        pltpu.make_async_copy(wd_hbm.at[:, :, pl.ds(pl.multiple_of(cb * CB, CB), CB)], ring.at[slot],
                              w_sem.at[slot]).start()

    def wait_w(slot):
        pltpu.make_async_copy(ring.at[slot], ring.at[slot], w_sem.at[slot]).wait()

    for u in range(NSLOT):
        start_w13(u // NEXP, u % NEXP, u)

    cp_i.wait()
    cp_g.wait()
    ids_f = ids_v[...].astype(F32)
    gates_f = gates_v[...]
    meta[0, 0, 0:8, :] = jnp.concatenate([ids_f, ids_f], axis=1)
    meta[0, 0, 8:16, :] = jnp.concatenate([gates_f, gates_f], axis=1)
    cp_x[0].wait()
    cp_x[1].wait()
    pl.semaphore_wait(barrier, len(PEERS))

    def rows(k, c, s, h):
        return xs.at[k, c, pl.ds(s * TOK + h * HALF, HALF)]

    def row_copy(k, src, dst, c, s):
        return remote(rows(k, *src), rows(k, *dst), xsend.at[k, dst[0], dst[1], dst[2]],
                      xrecv.at[k, dst[0], dst[1], dst[2]], c, s)

    ROUTES = {}
    for c in (1, 2):
        for h in range(2):
            ROUTES[(c, 0, h)] = ((0, 0, h), c, 0)
    ROUTES[(3, 0, 1)] = ((1, 0, 1), 2, 0)
    ROUTES[(3, 0, 0)] = ((2, 0, 0), 1, 0)
    for c in range(4):
        for h in range(2):
            ROUTES[(c, 1, h)] = ((c, 0, h), 0, 1)

    def send_rows(k, *dst):
        src, c, s = ROUTES[dst]
        row_copy(k, src, dst, c, s).start()

    def wait_rows(k, *dst):
        src, c, s = ROUTES[dst]
        row_copy(k, src, dst, c, s).wait_recv()

    def send_own(k):
        send_rows(k, 1, 0, 1)
        send_rows(k, 2, 0, 0)
        send_rows(k, 1, 0, 0)
        send_rows(k, 2, 0, 1)
        send_rows(k, 0, 1, 0)
        send_rows(k, 0, 1, 1)

    def forward_first(k):
        wait_rows(k, 1, 0, 1)
        send_rows(k, 3, 0, 1)
        send_rows(k, 1, 1, 1)
        wait_rows(k, 2, 0, 0)
        send_rows(k, 3, 0, 0)
        send_rows(k, 2, 1, 0)

    def forward_second(k):
        wait_rows(k, 1, 0, 0)
        send_rows(k, 1, 1, 0)
        wait_rows(k, 2, 0, 1)
        send_rows(k, 2, 1, 1)

    def forward_third(k):
        for h in range(2):
            wait_rows(k, 3, 0, h)
            send_rows(k, 3, 1, h)

    meta_sends = []
    for i, (c, s) in enumerate(PEERS):
        cp = remote(meta.at[0, 0], meta.at[c, s], msend.at[i], mrecv.at[c, s], c, s)
        cp.start()
        meta_sends.append(cp)
    send_own(0)
    forward_first(0)
    send_own(1)

    for c, s in PEERS:
        remote(meta.at[c, s], meta.at[c, s], msend.at[0], mrecv.at[c, s], 0, 1).wait_recv()
    base = ((ex * 2 + ey) * 2 + ez) * NEXP
    sub8 = lax.broadcasted_iota(jnp.int32, (NEXP, 128), 0)
    lane8 = lax.broadcasted_iota(jnp.int32, (NEXP, 128), 1)
    mine = (sub8 + base).astype(F32)
    masks, gates = [], []
    for c in range(4):
        m = jnp.where(lane8[0:1] < TOK, meta[c, 0], meta[c, 1])
        mask = jnp.zeros((NEXP, 128), F32)
        gate = jnp.zeros((NEXP, 128), F32)
        for j in range(8):
            hit = m[j:j + 1, :] == mine
            mask += jnp.where(hit, 1.0, 0.0)
            gate += jnp.where(hit, m[8 + j:9 + j, :], 0.0)
        masks.append(mask)
        gates.append(gate)
    r_i = lax.broadcasted_iota(jnp.int32, (128, 128), 0)
    c_i = lax.broadcasted_iota(jnp.int32, (128, 128), 1)
    before = jnp.where((r_i < c_i) & ((r_i < TOK) == (c_i < TOK)), 1.0, 0.0).astype(BF16)
    rank = jnp.dot(jnp.concatenate(masks, axis=0).astype(BF16), before, preferred_element_type=F32)
    sub32 = lax.broadcasted_iota(jnp.int32, (2 * CAP, 128), 0).astype(F32)
    core_off = jnp.where(lane8 < TOK, 0.0, float(CAP))
    for c in range(4):
        code = jnp.where(masks[c] > 0.5, rank[c * NEXP:(c + 1) * NEXP] + core_off, -1.0)
        for e in range(NEXP):
            hit = sub32 == code[e:e + 1, :]
            pmat[c, 2 * CAP * e:2 * CAP * (e + 1), :] = jnp.where(hit, 1.0, 0.0).astype(BF16)
            gtmp[c, 2 * CAP * e:2 * CAP * (e + 1), :] = jnp.where(hit, gates[c][e:e + 1, :], 0.0)
    for c in range(4):
        gt = gtmp[c].T
        hi = gt.astype(BF16)
        rest = gt - hi.astype(F32)
        mid = rest.astype(BF16)
        gmat[c, 0:128, :] = hi
        gmat[c, 128:256, :] = mid
        gmat[c, 256:384, :] = (rest - mid.astype(F32)).astype(BF16)

    def gather(k, c):
        for h in range(2):
            if (c, 1, h) in ROUTES:
                wait_rows(k, c, 1, h)
        for nb in range(FFN // 512):
            cols = slice(nb * 512, (nb + 1) * 512)
            blk = jnp.dot(pmat[c], xs[k, c, :, cols], preferred_element_type=F32).astype(BF16)
            for e in range(NEXP):
                xe[k, e, 2 * CAP * c:2 * CAP * (c + 1), cols] = blk[2 * CAP * e:2 * CAP * (e + 1)]

    gather(0, 0)
    forward_second(0)
    gather(0, 1)
    gather(0, 2)
    forward_third(0)
    gather(0, 3)

    def refill(u, slot):
        nxt = u + NSLOT

        @pl.when(nxt < N13)
        def _():
            start_w13(nxt // NEXP, lax.rem(nxt, NEXP), slot)

        @pl.when((nxt >= N13) & (nxt < N13 + NCB))
        def _():
            start_w2(nxt - N13, slot)

    def up0(e, carry):
        slot = lax.rem(e, NSLOT)
        wait_w(slot)
        for q in range(8):
            hbuf[e, q] = jnp.dot(xe[0, e], ring[slot, q], preferred_element_type=F32)
        refill(e, slot)

        @pl.when(e == 0)
        def _():
            forward_first(1)

        @pl.when(e == 2)
        def _():
            forward_second(1)
            gather(1, 0)

        @pl.when(e == 5)
        def _():
            gather(1, 1)
            gather(1, 2)
            forward_third(1)

        return carry

    lax.fori_loop(0, NEXP, up0, 0)
    gather(1, 3)

    def up1(e, carry):
        u = e + NEXP
        slot = lax.rem(u, NSLOT)
        wait_w(slot)
        for q in range(4):
            h1 = hbuf[e, q] + jnp.dot(xe[1, e], ring[slot, q], preferred_element_type=F32)
            h3 = hbuf[e, 4 + q] + jnp.dot(xe[1, e], ring[slot, 4 + q], preferred_element_type=F32)
            act[e, :, q * CB:(q + 1) * CB] = (jax.nn.silu(h1) * h3).astype(BF16)
        refill(u, slot)
        return carry

    lax.fori_loop(0, NEXP, up1, 0)

    def d_copy(cb, g):
        return remote(hbuf.at[cb, g], drecv.at[cb, g], d_send.at[cb, g], d_recv.at[cb, g], 0, 1)

    def s2_copy(cb, h):
        return remote(hbuf.at[cb, 3, pl.ds(h * TOK, TOK)], r2.at[cb, pl.ds(h * TOK, TOK)],
                      s2_send.at[cb, h], s2_recv.at[cb, h], HOP1[h], 0)

    def s3_copy(cb, h):
        return remote(hbuf.at[cb, 2, pl.ds(h * TOK + HALF, HALF)], r3.at[cb, pl.ds(h * HALF, HALF)],
                      s3_send.at[cb, h], s3_recv.at[cb, h], HOP2[h], 0)

    def part(cb):
        slot = lax.rem(N13 + cb, NSLOT)
        wait_w(slot)
        for e in range(NEXP):
            o = jnp.dot(act[e], ring[slot, e], preferred_element_type=F32).astype(BF16)
            for c in range(4):
                obuf[c, 2 * CAP * e:2 * CAP * (e + 1), :] = o[2 * CAP * c:2 * CAP * (c + 1)]
        for c in (3, 1, 2, 0):
            t = jnp.dot(gmat[c], obuf[c], preferred_element_type=F32)
            t = t[0:128] + t[128:256] + t[256:384]
            for h in range(2):
                g = 0 if c in STAY[h] else 1
                place = (LEAVE if g else STAY)[h].index(c)
                at = pl.ds(h * TOK + place * HALF, HALF)
                hbuf[cb, 2 + g, at] = t[h * HALF:(h + 1) * HALF]
                hbuf[cb, g, at] = t[TOK + h * HALF:TOK + (h + 1) * HALF]
        d_copy(cb, 1).start()
        d_copy(cb, 0).start()

    def stage2(cb):
        d_copy(cb, 1).wait_recv()
        hbuf[cb, 3] = hbuf[cb, 3] + drecv[cb, 1]
        s2_copy(cb, 0).start()
        s2_copy(cb, 1).start()

    def down(cb, carry):
        part(cb)

        @pl.when(cb > 0)
        def _():
            stage2(cb - 1)

        return carry

    lax.fori_loop(0, NCB, down, 0)
    stage2(NCB - 1)

    def third(cb, carry):
        d_copy(cb, 0).wait_recv()
        for h in range(2):
            s2_copy(cb, h).wait_recv()
        hbuf[cb, 2] = (hbuf[cb, 2] + drecv[cb, 0]) + r2[cb]
        for h in range(2):
            s3_copy(cb, h).start()
        return carry

    lax.fori_loop(0, NCB, third, 0)

    def last(cb, carry):
        cols = pl.ds(pl.multiple_of(lax.rem(cb, 4) * CB, CB), CB)
        ycols = pl.ds(pl.multiple_of(cb * CB, CB), CB)
        for h in range(2):
            s3_copy(cb, h).wait_recv()
            at = pl.ds(h * HALF, HALF)
            xin = xs[cb // 4, 0, at, cols].astype(F32)
            y_ref[at, ycols] = (xin + (hbuf[cb, 2, pl.ds(h * TOK, HALF)] + r3[cb, at])).astype(BF16)
        return carry

    lax.fori_loop(0, NCB, last, 0)

    for cp in meta_sends:
        cp.wait_send()
    for k in range(2):
        for dst, (src, c, s) in ROUTES.items():
            row_copy(k, src, dst, c, s).wait_send()
    for cb in range(NCB):
        for i in range(2):
            d_copy(cb, i).wait_send()
            s2_copy(cb, i).wait_send()
            s3_copy(cb, i).wait_send()


def solution(mesh):
    def local_layer(x_loc, ids_loc, gates_loc, w_g, w_u, w_d):
        w_g = w_g.reshape(NEXP, 2, FFN, FFN)
        w_u = w_u.reshape(NEXP, 2, FFN, FFN)
        any_spec = pl.BlockSpec(memory_space=pl.ANY)
        dma = pltpu.SemaphoreType.DMA
        return pl.pallas_call(
            kernel,
            out_shape=jax.ShapeDtypeStruct((TOK, HID), BF16),
            in_specs=[any_spec] * 6,
            out_specs=pl.BlockSpec(memory_space=pltpu.VMEM),
            scratch_shapes=[
                pltpu.VMEM((NSLOT, NEXP, FFN, CB), BF16),
                pltpu.VMEM((2, 4, 2 * TOK, FFN), BF16),
                pltpu.VMEM((2, NEXP, 8 * CAP, FFN), BF16),
                pltpu.VMEM((NEXP, 8, 8 * CAP, CB), F32),
                pltpu.VMEM((NEXP, 8 * CAP, FFN), BF16),
                pltpu.VMEM((NCB, 2, 2 * TOK, CB), F32),
                pltpu.VMEM((NCB, 2 * TOK, CB), F32),
                pltpu.VMEM((NCB, TOK, CB), F32),
                pltpu.VMEM((4, 2 * CAP * NEXP, 128), BF16),
                pltpu.VMEM((4, 2 * CAP * NEXP, 128), F32),
                pltpu.VMEM((4, 384, 2 * CAP * NEXP), BF16),
                pltpu.VMEM((4, 2 * CAP * NEXP, CB), BF16),
                pltpu.VMEM((8, TOK), jnp.int32),
                pltpu.VMEM((8, TOK), F32),
                pltpu.VMEM((4, 2, 16, 128), F32),
                dma((NSLOT,)),
                dma((4,)),
                dma((2, 4, 2, 2)),
                dma((2, 4, 2, 2)),
                dma((7,)),
                dma((4, 2)),
                dma((NCB, 2)),
                dma((NCB, 2)),
                dma((NCB, 2)),
                dma((NCB, 2)),
                dma((NCB, 2)),
                dma((NCB, 2)),
            ],
            compiler_params=pltpu.CompilerParams(collective_id=0, has_side_effects=True,
                                                 vmem_limit_bytes=67043328),
            name='moe_decode',
        )(x_loc, ids_loc.T, gates_loc.T, w_g, w_u, w_d)

    tok_spec = P(TOKEN_AXES, None)
    w_spec = P(EXPERT_AXES, None, None)
    return jax.shard_map(local_layer, mesh=mesh, in_specs=(tok_spec, tok_spec, tok_spec, w_spec, w_spec, w_spec), out_specs=tok_spec, check_vma=False)
```

time: 186 us -> 52.2 us (0.28)
  blocking collectives: 52.8 us -> 0 us
  matrix products: 51.2 us -> 0 us
  Pallas kernels: 0 us -> 50.4 us
  waiting for transfers between devices: 47.8 us -> 0 us
  local copies, waits for them, and re-layouts: 22.1 us -> 1.67 us
  other arithmetic: 8.04 us -> 0 us
  starting transfers between devices: 3.41 us -> 0 us
    all_to_all x1 -> x0, blocking collectives: 52.8 us -> none  [local_layer(): recv_buf = lax.all_to_all(send_buf, EXPERT_AXES, 0, 0)]
    dot_general x3 -> x0, matrix products: 51.2 us -> none  [the longest x1 18.3 us: local_layer(): jnp.einsum('slch,lhf->slcf', recv_buf, w_u, preferred_element_type=jnp.fl...]
    pallas_call x0 -> x1, Pallas kernels: none -> 50.4 us  [local_layer(): pl.pallas_call(kernel, out_shape=jax.ShapeDtypeStruct((TOK, HID), BF16),...]
    all_to_all x1 -> x0, waiting for transfers between devices: 47.8 us -> none  [local_layer(): back_buf = lax.all_to_all(exp_out, EXPERT_AXES, 0, 0)]
    gather x2 -> x0, local copies, waits for them, and re-layouts: 13.2 us -> none  [the longest x1 7.13 us: local_layer(): jnp.take(back_flat, slot_idx, axis=0).reshape(tok_dev, top_k, hid_dim)]
    convert_element_type x1 -> x0, local copies, waits for them, and re-layouts: 4.7 us -> none  [local_layer(): jnp.einsum('slcf,lfh->slch', act_bf, w_d, preferred_element_type=jnp.floa...]
    all_to_all x1 -> x0, starting transfers between devices: 3.41 us -> none  [local_layer(): back_buf = lax.all_to_all(exp_out, EXPERT_AXES, 0, 0)]
    select_n x3 -> x0, other arithmetic: 2.65 us -> none  [the longest x1 2.63 us: local_layer(): jnp.take(x_loc, slot_tok, axis=0).reshape(n_dev, n_local, cap_slot, hid_dim)]
  transfers between devices with their start and end apart: 1 -> 0, of which waited for: 1 -> 0; matrix products, arithmetic and copies ran while one was open for 0% -> 0% of each run, Pallas kernels for 0% -> 0%
where the time goes in v2:
time: 52.2 us; the launch traced here: 52.1 us
  Pallas kernels  50.4 us (97%)
  local copies, waits for them, and re-layouts  1.67 us (3%)
    pallas_call x1, Pallas kernels, local_layer(): pl.pallas_call(kernel, out_shape=jax.ShapeDtypeStruct((TOK, HID), BF16),...  50.4 us
    unnamed x1, local copies, waits for them, and re-layouts  1.67 us

profile of v2, /device:TPU:0, one launch (start us, length us, event | category | flops | bytes accessed | tf_op | source)
XLA Modules:
  0.0 52.1 jit_solution(276163948397280231)
XLA Ops:
  0.0 50.4 %moe_decode.1 = bf16[64,2048]{1,0:T(8,128)(2,1)} custom-call(bf16[64,2048]{1,0:T(8,128)(2,1)} %x_hbm.1, s32[8,64]{1,0:T(8,128)} %bitcast.6, f32[8,64]{1,0:T(8,128)} %bitcast.7, bf16[8,2,1024,1024]{3,2,1,0:T(8,128)(2,1)} %bitcast.4, bf16[8,2,1024,1024]{3,2,1,0:T(8,128)(2,1)} %bitcast.5, bf16[8,1024,2048]{2,1,0:T(8,128)(2,1)} %wd_hbm.1), custom_call_target="tpu_custom_call" | custom-call | tf_op jit(solution)/shard_map/moe_decode/pallas_call | solution.py:337
  50.4 1.7 %copy.8 = bf16[64,2048]{1,0:T(8,128)(2,1)} copy(bf16[64,2048]{1,0:T(8,128)(2,1)} %moe_decode.1) | data formatting | bytes 524288

commit v3 on v2

--- a/solution.py
+++ b/solution.py
@@ -54,16 +54,19 @@
 
     def start_w13(k, e, slot):
         for i, w_hbm in enumerate((wg_hbm, wu_hbm)):
-            for q in range(4):
-                pltpu.make_async_copy(w_hbm.at[e, k, :, pl.ds(q * CB, CB)], ring.at[slot, 4 * i + q],
-                                      w_sem.at[slot]).start()
+            pltpu.make_async_copy(w_hbm.at[e, k], ring.at[slot, i], w_sem.at[slot]).start()
 
     def start_w2(cb, slot):
-        pltpu.make_async_copy(wd_hbm.at[:, :, pl.ds(pl.multiple_of(cb * CB, CB), CB)], ring.at[slot],
-                              w_sem.at[slot]).start()
+        cols = pl.ds(pl.multiple_of(cb * CB, CB), CB)
+        for e in range(NEXP):
+            pltpu.make_async_copy(wd_hbm.at[e, :, cols], ring.at[slot, e // 4, :, pl.ds(e % 4 * CB, CB)],
+                                  w_sem.at[slot]).start()
 
     def wait_w(slot):
         pltpu.make_async_copy(ring.at[slot], ring.at[slot], w_sem.at[slot]).wait()
+
+    def wcols(slot, i):
+        return ring[slot, i // 4, :, i % 4 * CB:(i % 4 + 1) * CB]
 
     for u in range(NSLOT):
         start_w13(u // NEXP, u % NEXP, u)
@@ -103,9 +106,11 @@
         src, c, s = ROUTES[dst]
         row_copy(k, src, dst, c, s).wait_recv()
 
-    def send_own(k):
+    def send_first(k):
         send_rows(k, 1, 0, 1)
         send_rows(k, 2, 0, 0)
+
+    def send_second(k):
         send_rows(k, 1, 0, 0)
         send_rows(k, 2, 0, 1)
         send_rows(k, 0, 1, 0)
@@ -135,9 +140,11 @@
         cp = remote(meta.at[0, 0], meta.at[c, s], msend.at[i], mrecv.at[c, s], c, s)
         cp.start()
         meta_sends.append(cp)
-    send_own(0)
+    send_first(0)
+    send_second(0)
+    send_first(1)
     forward_first(0)
-    send_own(1)
+    send_second(1)
 
     for c, s in PEERS:
         remote(meta.at[c, s], meta.at[c, s], msend.at[0], mrecv.at[c, s], 0, 1).wait_recv()
@@ -191,6 +198,7 @@
     forward_second(0)
     gather(0, 1)
     gather(0, 2)
+    forward_first(1)
     forward_third(0)
     gather(0, 3)
 
@@ -209,23 +217,22 @@
         slot = lax.rem(e, NSLOT)
         wait_w(slot)
         for q in range(8):
-            hbuf[e, q] = jnp.dot(xe[0, e], ring[slot, q], preferred_element_type=F32)
+            hbuf[e, q] = jnp.dot(xe[0, e], wcols(slot, q), preferred_element_type=F32)
         refill(e, slot)
 
         @pl.when(e == 0)
         def _():
-            forward_first(1)
+            forward_second(1)
 
         @pl.when(e == 2)
         def _():
-            forward_second(1)
+            forward_third(1)
             gather(1, 0)
 
-        @pl.when(e == 5)
+        @pl.when(e == 4)
         def _():
             gather(1, 1)
             gather(1, 2)
-            forward_third(1)
 
         return carry
 
@@ -237,8 +244,8 @@
         slot = lax.rem(u, NSLOT)
         wait_w(slot)
         for q in range(4):
-            h1 = hbuf[e, q] + jnp.dot(xe[1, e], ring[slot, q], preferred_element_type=F32)
-            h3 = hbuf[e, 4 + q] + jnp.dot(xe[1, e], ring[slot, 4 + q], preferred_element_type=F32)
+            h1 = hbuf[e, q] + jnp.dot(xe[1, e], wcols(slot, q), preferred_element_type=F32)
+            h3 = hbuf[e, 4 + q] + jnp.dot(xe[1, e], wcols(slot, 4 + q), preferred_element_type=F32)
             act[e, :, q * CB:(q + 1) * CB] = (jax.nn.silu(h1) * h3).astype(BF16)
         refill(u, slot)
         return carry
@@ -260,7 +267,7 @@
         slot = lax.rem(N13 + cb, NSLOT)
         wait_w(slot)
         for e in range(NEXP):
-            o = jnp.dot(act[e], ring[slot, e], preferred_element_type=F32).astype(BF16)
+            o = jnp.dot(act[e], wcols(slot, e), preferred_element_type=F32).astype(BF16)
             for c in range(4):
                 obuf[c, 2 * CAP * e:2 * CAP * (e + 1), :] = o[2 * CAP * c:2 * CAP * (c + 1)]
         for c in (3, 1, 2, 0):
@@ -336,11 +343,11 @@
         dma = pltpu.SemaphoreType.DMA
         return pl.pallas_call(
             kernel,
-            out_shape=jax.ShapeDtypeStruct((TOK, HID), BF16),
+            out_shape=pltpu.VMEM((TOK, HID), BF16),
             in_specs=[any_spec] * 6,
             out_specs=pl.BlockSpec(memory_space=pltpu.VMEM),
             scratch_shapes=[
-                pltpu.VMEM((NSLOT, NEXP, FFN, CB), BF16),
+                pltpu.VMEM((NSLOT, 2, FFN, FFN), BF16),
                 pltpu.VMEM((2, 4, 2 * TOK, FFN), BF16),
                 pltpu.VMEM((2, NEXP, 8 * CAP, FFN), BF16),
                 pltpu.VMEM((NEXP, 8, 8 * CAP, CB), F32),
@@ -369,7 +376,7 @@
                 dma((NCB, 2)),
             ],
             compiler_params=pltpu.CompilerParams(collective_id=0, has_side_effects=True,
-                                                 vmem_limit_bytes=67043328),
+                                                 vmem_limit_bytes=66000000),
             name='moe_decode',
         )(x_loc, ids_loc.T, gates_loc.T, w_g, w_u, w_d)
 

time: 52.2 us -> 52.2 us (level)
  Pallas kernels: 50.4 us -> 51.4 us
  local copies, waits for them, and re-layouts: 1.67 us -> 0.71 us
    pallas_call x1, Pallas kernels: 50.4 us -> 51.4 us  [local_layer(): pl.pallas_call(kernel, out_shape=pltpu.VMEM((TOK, HID), BF16), in_specs=[...]
    unnamed x1, local copies, waits for them, and re-layouts: 1.67 us -> 0.71 us
where the time goes in v3:
time: 52.2 us; the launch traced here: 52.1 us
  Pallas kernels  51.4 us (98%)
  local copies, waits for them, and re-layouts  0.71 us (1%)
    pallas_call x1, Pallas kernels, local_layer(): pl.pallas_call(kernel, out_shape=pltpu.VMEM((TOK, HID), BF16), in_specs=[...  51.4 us

profile of v3, /device:TPU:0, one launch (start us, length us, event | category | flops | bytes accessed | tf_op | source)
XLA Modules:
  0.0 52.1 jit_solution(8718075965007686606)
XLA Ops:
  0.0 51.4 %moe_decode.1 = bf16[64,2048]{1,0:T(8,128)(2,1)S(1)} custom-call(bf16[64,2048]{1,0:T(8,128)(2,1)} %x_hbm.1, s32[8,64]{1,0:T(8,128)} %bitcast.6, f32[8,64]{1,0:T(8,128)} %bitcast.7, bf16[8,2,1024,1024]{3,2,1,0:T(8,128)(2,1)} %bitcast.4, bf16[8,2,1024,1024]{3,2,1,0:T(8,128)(2,1)} %bitcast.5, bf16[8,1024,2048]{2,1,0:T(8,128)(2,1)} %wd_hbm.1), custom_call_target="tpu_custom_call" | custom-call | tf_op jit(solution)/shard_map/moe_decode/pallas_call | solution.py:344
  51.4 0.7 %copy.8 = bf16[64,2048]{1,0:T(8,128)(2,1)} copy(bf16[64,2048]{1,0:T(8,128)(2,1)S(1)} %moe_decode.1) | data formatting | bytes 524288

commit v4 on v3

--- a/solution.py
+++ b/solution.py
@@ -17,7 +17,7 @@
 FFN = 1024
 NEXP = 8
 CAP = 16
-NSLOT = 9
+NSLOT = 10
 CB = 256
 NCB = HID // CB
 N13 = 2 * NEXP
@@ -54,22 +54,27 @@
 
     def start_w13(k, e, slot):
         for i, w_hbm in enumerate((wg_hbm, wu_hbm)):
-            pltpu.make_async_copy(w_hbm.at[e, k], ring.at[slot, i], w_sem.at[slot]).start()
+            for q in range(4):
+                pltpu.make_async_copy(w_hbm.at[e, k, :, pl.ds(q * CB, CB)], ring.at[slot, 4 * i + q],
+                                      w_sem.at[slot]).start()
 
     def start_w2(cb, slot):
         cols = pl.ds(pl.multiple_of(cb * CB, CB), CB)
         for e in range(NEXP):
-            pltpu.make_async_copy(wd_hbm.at[e, :, cols], ring.at[slot, e // 4, :, pl.ds(e % 4 * CB, CB)],
+            pltpu.make_async_copy(wd_hbm.at[e, :, cols], ring.at[slot, e],
                                   w_sem.at[slot]).start()
 
     def wait_w(slot):
         pltpu.make_async_copy(ring.at[slot], ring.at[slot], w_sem.at[slot]).wait()
 
     def wcols(slot, i):
-        return ring[slot, i // 4, :, i % 4 * CB:(i % 4 + 1) * CB]
-
-    for u in range(NSLOT):
-        start_w13(u // NEXP, u % NEXP, u)
+        return ring[slot, i]
+
+    def start_units(first, last):
+        for u in range(first, last):
+            start_w13(u // NEXP, u % NEXP, u)
+
+    start_units(0, 4)
 
     cp_i.wait()
     cp_g.wait()
@@ -142,8 +147,9 @@
         meta_sends.append(cp)
     send_first(0)
     send_second(0)
+    forward_first(0)
+    start_units(4, 6)
     send_first(1)
-    forward_first(0)
     send_second(1)
 
     for c, s in PEERS:
@@ -196,9 +202,10 @@
 
     gather(0, 0)
     forward_second(0)
+    start_units(6, 8)
     gather(0, 1)
     gather(0, 2)
-    forward_first(1)
+    start_units(8, NSLOT)
     forward_third(0)
     gather(0, 3)
 
@@ -222,17 +229,18 @@
 
         @pl.when(e == 0)
         def _():
+            forward_first(1)
+
+        @pl.when(e == 2)
+        def _():
             forward_second(1)
-
-        @pl.when(e == 2)
-        def _():
-            forward_third(1)
             gather(1, 0)
 
-        @pl.when(e == 4)
+        @pl.when(e == 5)
         def _():
             gather(1, 1)
             gather(1, 2)
+            forward_third(1)
 
         return carry
 
@@ -347,7 +355,7 @@
             in_specs=[any_spec] * 6,
             out_specs=pl.BlockSpec(memory_space=pltpu.VMEM),
             scratch_shapes=[
-                pltpu.VMEM((NSLOT, 2, FFN, FFN), BF16),
+                pltpu.VMEM((NSLOT, NEXP, FFN, CB), BF16),
                 pltpu.VMEM((2, 4, 2 * TOK, FFN), BF16),
                 pltpu.VMEM((2, NEXP, 8 * CAP, FFN), BF16),
                 pltpu.VMEM((NEXP, 8, 8 * CAP, CB), F32),

time: 52.2 us -> 50.5 us (0.967)
  Pallas kernels: 51.4 us -> 49.7 us
    pallas_call x1, Pallas kernels: 51.4 us -> 49.7 us  [local_layer(): pl.pallas_call(kernel, out_shape=pltpu.VMEM((TOK, HID), BF16), in_specs=[...]
where the time goes in v4:
time: 50.5 us; the launch traced here: 50.4 us
  Pallas kernels  49.7 us (98%)
  local copies, waits for them, and re-layouts  0.71 us (1%)
    pallas_call x1, Pallas kernels, local_layer(): pl.pallas_call(kernel, out_shape=pltpu.VMEM((TOK, HID), BF16), in_specs=[...  49.7 us

profile of v4, /device:TPU:0, one launch (start us, length us, event | category | flops | bytes accessed | tf_op | source)
XLA Modules:
  0.0 50.4 jit_solution(4659194172250591810)
XLA Ops:
  0.0 49.7 %moe_decode.1 = bf16[64,2048]{1,0:T(8,128)(2,1)S(1)} custom-call(bf16[64,2048]{1,0:T(8,128)(2,1)} %x_hbm.1, s32[8,64]{1,0:T(8,128)} %bitcast.6, f32[8,64]{1,0:T(8,128)} %bitcast.7, bf16[8,2,1024,1024]{3,2,1,0:T(8,128)(2,1)} %bitcast.4, bf16[8,2,1024,1024]{3,2,1,0:T(8,128)(2,1)} %bitcast.5, bf16[8,1024,2048]{2,1,0:T(8,128)(2,1)} %wd_hbm.1), custom_call_target="tpu_custom_call" | custom-call | tf_op jit(solution)/shard_map/moe_decode/pallas_call | solution.py:352
  49.7 0.7 %copy.8 = bf16[64,2048]{1,0:T(8,128)(2,1)} copy(bf16[64,2048]{1,0:T(8,128)(2,1)S(1)} %moe_decode.1) | data formatting | bytes 524288

commit v5 on v4

--- a/solution.py
+++ b/solution.py
@@ -13,6 +13,7 @@
 
 TOK = 64
 HALF = TOK // 2
+Q = TOK // 4
 HID = 2048
 FFN = 1024
 NEXP = 8
@@ -31,7 +32,7 @@
 
 def kernel(x_hbm, ids_hbm, gates_hbm, wg_hbm, wu_hbm, wd_hbm, y_ref,
            ring, xs, xe, hbuf, act, drecv, r2, r3, pmat, gtmp, gmat, obuf, ids_v, gates_v, meta,
-           w_sem, loc_sem, xsend, xrecv, msend, mrecv, d_send, d_recv, s2_send, s2_recv, s3_send, s3_recv):
+           w_sem, loc_sem, xsend, xa, xb, xd, drows, msend, mrecv, d_send, d_recv, d_stay, s2_send, s2_recv, s3_send, s3_recv):
     ez, ey, ex = lax.axis_index('ez'), lax.axis_index('ey'), lax.axis_index('ex')
 
     def dev(c, s):
@@ -74,99 +75,88 @@
         for u in range(first, last):
             start_w13(u // NEXP, u % NEXP, u)
 
-    start_units(0, 4)
+    start_units(0, 6)
 
     cp_i.wait()
     cp_g.wait()
     ids_f = ids_v[...].astype(F32)
     gates_f = gates_v[...]
-    meta[0, 0, 0:8, :] = jnp.concatenate([ids_f, ids_f], axis=1)
-    meta[0, 0, 8:16, :] = jnp.concatenate([gates_f, gates_f], axis=1)
+    meta[0] = jnp.concatenate([ids_f, gates_f], axis=1)
     cp_x[0].wait()
-    cp_x[1].wait()
     pl.semaphore_wait(barrier, len(PEERS))
 
-    def rows(k, c, s, h):
-        return xs.at[k, c, pl.ds(s * TOK + h * HALF, HALF)]
-
-    def row_copy(k, src, dst, c, s):
-        return remote(rows(k, *src), rows(k, *dst), xsend.at[k, dst[0], dst[1], dst[2]],
-                      xrecv.at[k, dst[0], dst[1], dst[2]], c, s)
-
-    ROUTES = {}
-    for c in (1, 2):
-        for h in range(2):
-            ROUTES[(c, 0, h)] = ((0, 0, h), c, 0)
-    ROUTES[(3, 0, 1)] = ((1, 0, 1), 2, 0)
-    ROUTES[(3, 0, 0)] = ((2, 0, 0), 1, 0)
-    for c in range(4):
-        for h in range(2):
-            ROUTES[(c, 1, h)] = ((c, 0, h), 0, 1)
-
-    def send_rows(k, *dst):
-        src, c, s = ROUTES[dst]
-        row_copy(k, src, dst, c, s).start()
-
-    def wait_rows(k, *dst):
-        src, c, s = ROUTES[dst]
-        row_copy(k, src, dst, c, s).wait_recv()
+    def send_rows(k, src, dst, first, count, rsem, c, s):
+        at = lambda cc, ss: xs.at[k, cc, pl.ds(ss * TOK + first, count)]
+        remote(at(*src), at(*dst), xsend.at[0], rsem, c, s).start()
+
+    def wait_all(ref, sem):
+        pltpu.make_async_copy(ref, ref, sem).wait()
+
+    def wait_rows(k, c, first, count, sem):
+        wait_all(xs.at[k, c, pl.ds(first, count)], sem)
+
+    def across(k, c, first, count):
+        send_rows(k, (c, 0), (c, 1), first, count, drows.at[k, c // 3], 0, 1)
+
+    def fwd_first(c, i):
+        return (HALF if c == 1 else 0) + i * Q
 
     def send_first(k):
-        send_rows(k, 1, 0, 1)
-        send_rows(k, 2, 0, 0)
+        for i in range(2):
+            for c in (1, 2):
+                send_rows(k, (0, 0), (c, 0), fwd_first(c, i), Q, xa.at[k, c - 1, i], c, 0)
 
     def send_second(k):
-        send_rows(k, 1, 0, 0)
-        send_rows(k, 2, 0, 1)
-        send_rows(k, 0, 1, 0)
-        send_rows(k, 0, 1, 1)
+        for c in (1, 2):
+            send_rows(k, (0, 0), (c, 0), HALF - fwd_first(c, 0), HALF, xb.at[k, c - 1], c, 0)
+        across(k, 0, 0, TOK)
 
     def forward_first(k):
-        wait_rows(k, 1, 0, 1)
-        send_rows(k, 3, 0, 1)
-        send_rows(k, 1, 1, 1)
-        wait_rows(k, 2, 0, 0)
-        send_rows(k, 3, 0, 0)
-        send_rows(k, 2, 1, 0)
+        for i in range(2):
+            for c in (1, 2):
+                wait_rows(k, c, fwd_first(c, i), Q, xa.at[k, c - 1, i])
+                send_rows(k, (c, 0), (3, 0), fwd_first(c, i), Q, xd.at[k, c - 1, i], 3 - c, 0)
+        for c in (1, 2):
+            across(k, c, fwd_first(c, 0), HALF)
 
     def forward_second(k):
-        wait_rows(k, 1, 0, 0)
-        send_rows(k, 1, 1, 0)
-        wait_rows(k, 2, 0, 1)
-        send_rows(k, 2, 1, 1)
+        for c in (1, 2):
+            first = HALF - fwd_first(c, 0)
+            wait_rows(k, c, first, HALF, xb.at[k, c - 1])
+            across(k, c, first, HALF)
 
     def forward_third(k):
-        for h in range(2):
-            wait_rows(k, 3, 0, h)
-            send_rows(k, 3, 1, h)
-
-    meta_sends = []
-    for i, (c, s) in enumerate(PEERS):
-        cp = remote(meta.at[0, 0], meta.at[c, s], msend.at[i], mrecv.at[c, s], c, s)
-        cp.start()
-        meta_sends.append(cp)
+        for i in range(2):
+            for c in (1, 2):
+                wait_rows(k, 3, fwd_first(c, i), Q, xd.at[k, c - 1, i])
+                across(k, 3, fwd_first(c, i), Q)
+
     send_first(0)
+    for c, s in PEERS:
+        remote(meta.at[0], meta.at[2 * c + s], msend.at[0], mrecv.at[0], c, s).start()
     send_second(0)
     forward_first(0)
-    start_units(4, 6)
+    start_units(6, NSLOT)
+    cp_x[1].wait()
     send_first(1)
     send_second(1)
 
-    for c, s in PEERS:
-        remote(meta.at[c, s], meta.at[c, s], msend.at[0], mrecv.at[c, s], 0, 1).wait_recv()
+    wait_all(meta.at[pl.ds(1, 7)], mrecv.at[0])
     base = ((ex * 2 + ey) * 2 + ez) * NEXP
     sub8 = lax.broadcasted_iota(jnp.int32, (NEXP, 128), 0)
     lane8 = lax.broadcasted_iota(jnp.int32, (NEXP, 128), 1)
     mine = (sub8 + base).astype(F32)
     masks, gates = [], []
     for c in range(4):
-        m = jnp.where(lane8[0:1] < TOK, meta[c, 0], meta[c, 1])
+        m0, m1 = meta[2 * c], meta[2 * c + 1]
+        ids_c = jnp.where(lane8 < TOK, m0, pltpu.roll(m1, TOK, 1))
+        gates_c = jnp.where(lane8 < TOK, pltpu.roll(m0, TOK, 1), m1)
         mask = jnp.zeros((NEXP, 128), F32)
         gate = jnp.zeros((NEXP, 128), F32)
         for j in range(8):
-            hit = m[j:j + 1, :] == mine
+            hit = ids_c[j:j + 1, :] == mine
             mask += jnp.where(hit, 1.0, 0.0)
-            gate += jnp.where(hit, m[8 + j:9 + j, :], 0.0)
+            gate += jnp.where(hit, gates_c[j:j + 1, :], 0.0)
         masks.append(mask)
         gates.append(gate)
     r_i = lax.broadcasted_iota(jnp.int32, (128, 128), 0)
@@ -191,23 +181,25 @@
         gmat[c, 256:384, :] = (rest - mid.astype(F32)).astype(BF16)
 
     def gather(k, c):
-        for h in range(2):
-            if (c, 1, h) in ROUTES:
-                wait_rows(k, c, 1, h)
         for nb in range(FFN // 512):
             cols = slice(nb * 512, (nb + 1) * 512)
             blk = jnp.dot(pmat[c], xs[k, c, :, cols], preferred_element_type=F32).astype(BF16)
             for e in range(NEXP):
                 xe[k, e, 2 * CAP * c:2 * CAP * (c + 1), cols] = blk[2 * CAP * e:2 * CAP * (e + 1)]
 
-    gather(0, 0)
+    def gather_near(k):
+        wait_all(xs.at[k, pl.ds(0, 3), pl.ds(TOK, TOK)], drows.at[k, 0])
+        for c in range(3):
+            gather(k, c)
+
+    def gather_far(k):
+        wait_all(xs.at[k, 3, pl.ds(TOK, TOK)], drows.at[k, 1])
+        gather(k, 3)
+
     forward_second(0)
-    start_units(6, 8)
-    gather(0, 1)
-    gather(0, 2)
-    start_units(8, NSLOT)
+    gather_near(0)
     forward_third(0)
-    gather(0, 3)
+    gather_far(0)
 
     def refill(u, slot):
         nxt = u + NSLOT
@@ -220,32 +212,33 @@
         def _():
             start_w2(nxt - N13, slot)
 
-    def up0(e, carry):
-        slot = lax.rem(e, NSLOT)
-        wait_w(slot)
-        for q in range(8):
-            hbuf[e, q] = jnp.dot(xe[0, e], wcols(slot, q), preferred_element_type=F32)
-        refill(e, slot)
-
-        @pl.when(e == 0)
+    def up0(i, carry):
+        for j in range(2):
+            wait_w(lax.rem(2 * i + j, NSLOT))
+        for j in range(2):
+            e = 2 * i + j
+            for q in range(8):
+                hbuf[e, q] = jnp.dot(xe[0, e], wcols(lax.rem(e, NSLOT), q), preferred_element_type=F32)
+        for j in range(2):
+            refill(2 * i + j, lax.rem(2 * i + j, NSLOT))
+
+        @pl.when(i == 0)
         def _():
             forward_first(1)
 
-        @pl.when(e == 2)
+        @pl.when(i == 1)
         def _():
             forward_second(1)
-            gather(1, 0)
-
-        @pl.when(e == 5)
-        def _():
-            gather(1, 1)
-            gather(1, 2)
+
+        @pl.when(i == 2)
+        def _():
+            gather_near(1)
             forward_third(1)
 
         return carry
 
-    lax.fori_loop(0, NEXP, up0, 0)
-    gather(1, 3)
+    lax.fori_loop(0, NEXP // 2, up0, 0)
+    gather_far(1)
 
     def up1(e, carry):
         u = e + NEXP
@@ -260,16 +253,20 @@
 
     lax.fori_loop(0, NEXP, up1, 0)
 
+    wait_all(hbuf.at[pl.ds(0, 2), pl.ds(0, 7)], xsend.at[0])
+    wait_all(meta.at[pl.ds(1, 7)], msend.at[0])
+
     def d_copy(cb, g):
-        return remote(hbuf.at[cb, g], drecv.at[cb, g], d_send.at[cb, g], d_recv.at[cb, g], 0, 1)
+        return remote(hbuf.at[cb, g], drecv.at[cb, g], d_send.at[0], d_recv.at[cb] if g else d_stay.at[0], 0, 1)
 
     def s2_copy(cb, h):
         return remote(hbuf.at[cb, 3, pl.ds(h * TOK, TOK)], r2.at[cb, pl.ds(h * TOK, TOK)],
-                      s2_send.at[cb, h], s2_recv.at[cb, h], HOP1[h], 0)
-
-    def s3_copy(cb, h):
-        return remote(hbuf.at[cb, 2, pl.ds(h * TOK + HALF, HALF)], r3.at[cb, pl.ds(h * HALF, HALF)],
-                      s3_send.at[cb, h], s3_recv.at[cb, h], HOP2[h], 0)
+                      s2_send.at[0], s2_recv.at[cb // 2], HOP1[h], 0)
+
+    def s3_copy(i, h):
+        return remote(hbuf.at[pl.ds(2 * i, 2), 2, pl.ds(h * TOK + HALF, HALF)],
+                      r3.at[pl.ds(2 * i, 2), pl.ds(h * HALF, HALF)],
+                      s3_send.at[0], s3_recv.at[(i + 1) // (NCB // 2)], HOP2[h], 0)
 
     def part(cb):
         slot = lax.rem(N13 + cb, NSLOT)
@@ -308,39 +305,34 @@
     lax.fori_loop(0, NCB, down, 0)
     stage2(NCB - 1)
 
-    def third(cb, carry):
-        d_copy(cb, 0).wait_recv()
+    wait_all(drecv.at[:, 0], d_stay.at[0])
+
+    def third(i, carry):
+        pair = pl.ds(2 * i, 2)
+        wait_all(r2.at[pair], s2_recv.at[i])
+        hbuf[pair, 2] = (hbuf[pair, 2] + drecv[pair, 0]) + r2[pair]
         for h in range(2):
-            s2_copy(cb, h).wait_recv()
-        hbuf[cb, 2] = (hbuf[cb, 2] + drecv[cb, 0]) + r2[cb]
-        for h in range(2):
-            s3_copy(cb, h).start()
-        return carry
-
-    lax.fori_loop(0, NCB, third, 0)
+            s3_copy(i, h).start()
+        return carry
+
+    lax.fori_loop(0, NCB // 2, third, 0)
+    wait_all(drecv, d_send.at[0])
+    wait_all(r2, s2_send.at[0])
 
     def last(cb, carry):
         cols = pl.ds(pl.multiple_of(lax.rem(cb, 4) * CB, CB), CB)
         ycols = pl.ds(pl.multiple_of(cb * CB, CB), CB)
         for h in range(2):
-            s3_copy(cb, h).wait_recv()
             at = pl.ds(h * HALF, HALF)
             xin = xs[cb // 4, 0, at, cols].astype(F32)
             y_ref[at, ycols] = (xin + (hbuf[cb, 2, pl.ds(h * TOK, HALF)] + r3[cb, at])).astype(BF16)
         return carry
 
-    lax.fori_loop(0, NCB, last, 0)
-
-    for cp in meta_sends:
-        cp.wait_send()
-    for k in range(2):
-        for dst, (src, c, s) in ROUTES.items():
-            row_copy(k, src, dst, c, s).wait_send()
-    for cb in range(NCB):
-        for i in range(2):
-            d_copy(cb, i).wait_send()
-            s2_copy(cb, i).wait_send()
-            s3_copy(cb, i).wait_send()
+    wait_all(r3.at[pl.ds(0, NCB - 2)], s3_recv.at[0])
+    lax.fori_loop(0, NCB - 2, last, 0)
+    wait_all(r3.at[pl.ds(NCB - 2, 2)], s3_recv.at[1])
+    lax.fori_loop(NCB - 2, NCB, last, 0)
+    wait_all(r3, s3_send.at[0])
 
 
 def solution(mesh):
@@ -369,19 +361,23 @@
                 pltpu.VMEM((4, 2 * CAP * NEXP, CB), BF16),
                 pltpu.VMEM((8, TOK), jnp.int32),
                 pltpu.VMEM((8, TOK), F32),
-                pltpu.VMEM((4, 2, 16, 128), F32),
+                pltpu.VMEM((8, 8, 128), F32),
                 dma((NSLOT,)),
                 dma((4,)),
-                dma((2, 4, 2, 2)),
-                dma((2, 4, 2, 2)),
-                dma((7,)),
-                dma((4, 2)),
-                dma((NCB, 2)),
-                dma((NCB, 2)),
-                dma((NCB, 2)),
-                dma((NCB, 2)),
-                dma((NCB, 2)),
-                dma((NCB, 2)),
+                dma((1,)),
+                dma((2, 2, 2)),
+                dma((2, 2)),
+                dma((2, 2, 2)),
+                dma((2, 2)),
+                dma((1,)),
+                dma((1,)),
+                dma((1,)),
+                dma((NCB,)),
+                dma((1,)),
+                dma((1,)),
+                dma((NCB // 2,)),
+                dma((1,)),
+                dma((2,)),
             ],
             compiler_params=pltpu.CompilerParams(collective_id=0, has_side_effects=True,
                                                  vmem_limit_bytes=66000000),

time: 50.5 us -> 47.6 us (0.943)
  Pallas kernels: 49.7 us -> 46.8 us
    pallas_call x1, Pallas kernels: 49.7 us -> 46.8 us  [local_layer(): pl.pallas_call(kernel, out_shape=pltpu.VMEM((TOK, HID), BF16), in_specs=[...]
where the time goes in v5:
time: 47.6 us; the launch traced here: 47.5 us
  Pallas kernels  46.8 us (98%)
  local copies, waits for them, and re-layouts  0.71 us (1%)
    pallas_call x1, Pallas kernels, local_layer(): pl.pallas_call(kernel, out_shape=pltpu.VMEM((TOK, HID), BF16), in_specs=[...  46.8 us

profile of v5, /device:TPU:0, one launch (start us, length us, event | category | flops | bytes accessed | tf_op | source)
XLA Modules:
  0.0 47.5 jit_solution(10485816680280789781)
XLA Ops:
  0.0 46.8 %moe_decode.1 = bf16[64,2048]{1,0:T(8,128)(2,1)S(1)} custom-call(bf16[64,2048]{1,0:T(8,128)(2,1)} %x_hbm.1, s32[8,64]{1,0:T(8,128)} %bitcast.6, f32[8,64]{1,0:T(8,128)} %bitcast.7, bf16[8,2,1024,1024]{3,2,1,0:T(8,128)(2,1)} %bitcast.4, bf16[8,2,1024,1024]{3,2,1,0:T(8,128)(2,1)} %bitcast.5, bf16[8,1024,2048]{2,1,0:T(8,128)(2,1)} %wd_hbm.1), custom_call_target="tpu_custom_call" | custom-call | tf_op jit(solution)/shard_map/moe_decode/pallas_call | solution.py:344
  46.8 0.7 %copy.8 = bf16[64,2048]{1,0:T(8,128)(2,1)} copy(bf16[64,2048]{1,0:T(8,128)(2,1)S(1)} %moe_decode.1) | data formatting | bytes 524288

commit v6 on v5

--- a/solution.py
+++ b/solution.py
@@ -240,18 +240,29 @@
     lax.fori_loop(0, NEXP // 2, up0, 0)
     gather_far(1)
 
-    def up1(e, carry):
-        u = e + NEXP
-        slot = lax.rem(u, NSLOT)
-        wait_w(slot)
-        for q in range(4):
-            h1 = hbuf[e, q] + jnp.dot(xe[1, e], wcols(slot, q), preferred_element_type=F32)
-            h3 = hbuf[e, 4 + q] + jnp.dot(xe[1, e], wcols(slot, 4 + q), preferred_element_type=F32)
-            act[e, :, q * CB:(q + 1) * CB] = (jax.nn.silu(h1) * h3).astype(BF16)
-        refill(u, slot)
-        return carry
-
-    lax.fori_loop(0, NEXP, up1, 0)
+    def up1(first, count):
+        slots = [lax.rem(first + j + NEXP, NSLOT) for j in range(count)]
+        for slot in slots:
+            wait_w(slot)
+        for j, slot in enumerate(slots):
+            e = first + j
+            for q in range(4):
+                h1 = hbuf[e, q] + jnp.dot(xe[1, e], wcols(slot, q), preferred_element_type=F32)
+                h3 = hbuf[e, 4 + q] + jnp.dot(xe[1, e], wcols(slot, 4 + q), preferred_element_type=F32)
+                act[e, :, q * CB:(q + 1) * CB] = (jax.nn.silu(h1) * h3).astype(BF16)
+        for j, slot in enumerate(slots):
+            refill(first + j + NEXP, slot)
+
+    def up1_pair(i, carry):
+        up1(2 * i, 2)
+        return carry
+
+    def up1_one(e, carry):
+        up1(e, 1)
+        return carry
+
+    lax.fori_loop(0, NEXP // 2 - 1, up1_pair, 0)
+    lax.fori_loop(NEXP - 2, NEXP, up1_one, 0)
 
     wait_all(hbuf.at[pl.ds(0, 2), pl.ds(0, 7)], xsend.at[0])
     wait_all(meta.at[pl.ds(1, 7)], msend.at[0])

time: 47.6 us -> 47.6 us (level)
  no operation moved by 1% of the time
where the time goes in v6:
time: 47.6 us; the launch traced here: 47.5 us
  Pallas kernels  46.8 us (98%)
  local copies, waits for them, and re-layouts  0.71 us (1%)
    pallas_call x1, Pallas kernels, local_layer(): pl.pallas_call(kernel, out_shape=pltpu.VMEM((TOK, HID), BF16), in_specs=[...  46.8 us

profile of v6, /device:TPU:0, one launch (start us, length us, event | category | flops | bytes accessed | tf_op | source)
XLA Modules:
  0.0 47.5 jit_solution(10871479910831616266)
XLA Ops:
  0.0 46.8 %moe_decode.1 = bf16[64,2048]{1,0:T(8,128)(2,1)S(1)} custom-call(bf16[64,2048]{1,0:T(8,128)(2,1)} %x_hbm.1, s32[8,64]{1,0:T(8,128)} %bitcast.6, f32[8,64]{1,0:T(8,128)} %bitcast.7, bf16[8,2,1024,1024]{3,2,1,0:T(8,128)(2,1)} %bitcast.4, bf16[8,2,1024,1024]{3,2,1,0:T(8,128)(2,1)} %bitcast.5, bf16[8,1024,2048]{2,1,0:T(8,128)(2,1)} %wd_hbm.1), custom_call_target="tpu_custom_call" | custom-call | tf_op jit(solution)/shard_map/moe_decode/pallas_call | solution.py:355
  46.8 0.7 %copy.8 = bf16[64,2048]{1,0:T(8,128)(2,1)} copy(bf16[64,2048]{1,0:T(8,128)(2,1)S(1)} %moe_decode.1) | data formatting | bytes 524288
